TPU v7x, 256 devices: a whole 4x4x8 slice. The times are simulated.
256 devices in a mesh: row: 32 (over y_lo, z, core), col: 8 (over x, y_hi).
Axes of the slice: x: 4, y: 4 (y_hi: 2, y_lo: 2; y = y_hi * 2 + y_lo), z: 8, core: 2. Of those that a mesh axis runs over, the one named last changes fastest.
Arguments:
- queries: bfloat16 [32768, 1024], P(('col', 'row')), may hold values from -150 to 150
- keys: bfloat16 [32768, 128], P(('row', 'col')), may hold values from -5 to 5
- values: bfloat16 [32768, 128], P(('row', 'col')), may hold values from -6 to 6
- segment_ids: int32 [32768], replicated, may hold values from 0 to 7, never falling along the last dimension, each value on 1 to 8192 neighbouring positions
Outputs:
- attended: bfloat16 [32768, 1024], P(('col', 'row'))
All inputs are finite; a program needn't handle non-finite values.
Results may differ from a plain program's by a relative error of at most 0.013.
Values may be sent and summed in bfloat16 or wider, within the bound.
A program may use at most 128 MiB of HBM per device.

v0:
```python
import functools
import math

import jax
import jax.numpy as jnp
from jax import lax
from jax.sharding import PartitionSpec as P

HQ = 8
HD = 128


def sent_together(arrays, axis, dim, along):
    ends, at = ([], 0)
    for a in arrays[:-1]:
        at += a.shape[along]
        ends.append(at)
    both = jnp.concatenate(arrays, axis=along)
    return tuple(jnp.split(lax.all_gather(both, axis, axis=dim, tiled=True), ends, axis=along))


def over_pieces(array, axis):
    return lax.all_gather(array, axis).max(0)


def in_blocks(array, dim, peers):
    before, after = (array.shape[:dim], array.shape[dim + 1 :])
    return jnp.moveaxis(array.reshape(*before, peers, -1, *after), dim, 0)


def one_scatter(arrays, axis, dims):
    peers = lax.axis_size(axis)
    tiles = [in_blocks(a, dim, peers) for a, dim in zip(arrays, dims)]
    lines = jnp.concatenate([b.reshape(peers, -1) for b in tiles], axis=1)
    extent = max(16, -(-lines.shape[1] // 1024) * 8)
    lines = jnp.pad(lines, ((0, 0), (0, extent * 128 - lines.shape[1]))).reshape(-1, 128)
    ravelled, at, finished = (lax.psum_scatter(lines, axis, tiled=True).reshape(-1), 0, [])
    for b in tiles:
        part = b[0]
        finished.append(ravelled[at : at + part.size].reshape(part.shape))
        at += part.size
    return tuple(finished)


def keep_state(current):
    return current


def fold_block(running, query_mat, query_pos, query_seg, key_block, value_block, key_pos, key_seg):
    old_max, old_total, old_numer = running
    scale_factor = 1.0 / math.sqrt(query_mat.shape[2])
    total_rows = query_mat.shape[0]
    new_max, new_total, new_numer = ([], [], [])
    for query_lo in range(0, total_rows, 512):
        query_hi = min(total_rows, query_lo + 512)
        scores = (
            jnp.einsum(
                "qhd,kd->qhk",
                query_mat[query_lo:query_hi],
                key_block,
                preferred_element_type=jnp.float32,
            )
            * scale_factor
        )
        visible = (query_seg[query_lo:query_hi, None] == key_seg[None, :]) & (
            key_pos[None, :] <= query_pos[query_lo:query_hi, None]
        )
        visible = visible[:, None, :]
        block_max = jnp.max(jnp.where(visible, scores, -1e30), axis=2)
        merged_max = jnp.maximum(old_max[query_lo:query_hi], block_max)
        exp_terms = jnp.where(visible, jnp.exp(scores - merged_max[..., None]), 0.0)
        rescale = jnp.exp(old_max[query_lo:query_hi] - merged_max)
        new_max.append(merged_max)
        new_total.append(old_total[query_lo:query_hi] * rescale + jnp.sum(exp_terms, axis=2))
        product = jnp.einsum(
            "qhk,kd->qhd",
            exp_terms.astype(jnp.bfloat16),
            value_block,
            preferred_element_type=jnp.float32,
        )
        new_numer.append(old_numer[query_lo:query_hi] * rescale[..., None] + product)
    return (
        jnp.concatenate(new_max, axis=0),
        jnp.concatenate(new_total, axis=0),
        jnp.concatenate(new_numer, axis=0),
    )


def absorb_keys(
    running, shard_piece, offset, query_mat, query_pos, query_seg, segment_ids, key_base
):
    key_piece, value_piece = shard_piece
    piece_rows = key_piece.shape[0]
    latest = jnp.max(query_pos)
    for block_lo in range(0, piece_rows, 512):
        block_hi = min(piece_rows, block_lo + 512)
        block_width = block_hi - block_lo
        first_key = key_base + block_lo
        key_pos = first_key + jnp.arange(block_width, dtype=jnp.int32)
        key_seg = lax.dynamic_slice_in_dim(segment_ids, first_key, block_width, 0)
        update = functools.partial(
            fold_block,
            query_mat=query_mat,
            query_pos=query_pos,
            query_seg=query_seg,
            key_block=key_piece[block_lo:block_hi],
            value_block=value_piece[block_lo:block_hi],
            key_pos=key_pos,
            key_seg=key_seg,
        )
        running = lax.cond(key_pos[0] > latest, keep_state, update, running)
    return running


def per_device(queries, keys, values, segment_ids):
    shard_rows = queries.shape[0]
    n_row = lax.axis_size("row")
    n_col = lax.axis_size("col")
    row_index = lax.axis_index("row")
    col_index = lax.axis_index("col")
    gathered = lax.all_gather(queries, "row", axis=0, tiled=True)
    query_start = col_index * (n_row * shard_rows)
    key_base = row_index * (n_col * shard_rows)
    query_pos = query_start + jnp.arange(gathered.shape[0], dtype=jnp.int32)
    total_rows = gathered.shape[0]
    query_mat = gathered.reshape(total_rows, HQ, HD)
    query_seg = jnp.take(segment_ids, query_pos)
    initial = (
        jnp.full((total_rows, HQ), -1e30, jnp.float32),
        jnp.zeros((total_rows, HQ), jnp.float32),
        jnp.zeros((total_rows, HQ, HD), jnp.float32),
    )
    absorb = functools.partial(
        absorb_keys,
        query_mat=query_mat,
        query_pos=query_pos,
        query_seg=query_seg,
        segment_ids=segment_ids,
        key_base=key_base,
    )
    running = absorb(initial, sent_together((keys, values), "col", 0, 1), jnp.int32(0))
    peak = over_pieces(running[0].astype(jnp.bfloat16), "row").astype(jnp.float32)
    rescale = jnp.exp(running[0] - peak)
    best_numer, best_total = tuple(
        (
            part.astype(jnp.float32)
            for part in one_scatter(
                (
                    (running[2] * rescale[..., None]).astype(jnp.bfloat16),
                    (running[1] * rescale).astype(jnp.bfloat16),
                ),
                "row",
                (0, 0),
            )
        )
    )
    owned = best_numer / best_total[..., None]
    return owned.reshape(shard_rows, HQ * HD).astype(jnp.bfloat16)


def solution(mesh):
    in_specs = (P(("col", "row"), None), P(("row", "col"), None), P(("row", "col"), None), P())
    out_specs = P(("col", "row"), None)
    return jax.shard_map(
        per_device, mesh=mesh, in_specs=in_specs, out_specs=out_specs, check_vma=False
    )
```

profile of v0, /device:TPU:1, one launch (start us, length us, event | category | flops | bytes accessed | tf_op | source)
XLA Modules:
  0.0 650.9 jit_solution(11856465075678931986)
XLA Ops:
  6.5 1.8 copy.58
  9.3 23.0 %gather_fusion = s32[4096]{0:T(1024)S(1)} fusion(s32[32768]{0:T(1024)S(1)} %copy-done, s32[4096]{0:T(1024)S(1)} %broadcast_clamp_fusion), kind=kCustom, calls=%fused_computation | custom fusion | bytes 49152 | tf_op jit(solution)/shard_map/jit(_take)/gather | solution.py:127
  36.6 30.2 %all_gather.13 = bf16[1024,256]{1,0:T(8,128)(2,1)S(1)} all-gather(bf16[128,256]{1,0:T(8,128)(2,1)S(1)} %pad_maximum_fusion.1), channel_id=1, replica_groups=mesh['row'=32,'col'=8] {'col'}, dimensions={0}, use_global_device_ids=true | all-gather | bytes 589824 | tf_op jit(solution)/shard_map/all_gather | solution.py:19
  66.9 37.2 %all-gather.4.cloned.1.call-done = bf16[4096,1024]{0,1:T(8,128)(2,1)} async-done(((bf16[128,1024]{0,1:T(8,128)(2,1)}), bf16[4096,1024]{0,1:T(8,128)(2,1)}) %all-gather.4.cloned.1.call-update) | async-done | bytes 8388624 | tf_op jit(solution)/shard_map/all_gather | solution.py:121
  104.1 74.7 %conditional.2 = (f32[4096,8]{0,1:T(8,128)S(1)}, f32[4096,8]{0,1:T(8,128)S(1)}, f32[4096,8,128]{2,0,1:T(8,128)S(1)}) conditional(s32[]{:T(128)} %convert_element_type.95, (s32[4096]{0:T(1024)S(1)}, s32[512]{0:T(512)S(1)}, s32[512]{0:T(512)S(1)}, s32[4096]{0:T(1024)S(1)}, bf16[4096,8,128]{0,2,1:T(8,128)(2,1)}, ...), branch_computations={%region_1.18_spmd, %region_18.19_spmd} | conditional | flops 8785068032 | bytes 255430688 | solution.py:111
  104.1 2.0 compare_and_fusion
  106.1 11.9 %copy.59 = bf16[4096,8,128]{2,0,1:T(8,128)(2,1)} copy(bf16[4096,8,128]{0,2,1:T(8,128)(2,1)} %get-tuple-element.137) | data formatting | bytes 16777216 | tf_op jit(solution)/shard_map
  118.1 2.7 select_reduce_fusion.7
  120.8 1.7 fusion.1
  122.6 2.8 add_dynamic-update-slice_fusion.7
  125.4 2.7 select_reduce_fusion.6
  129.9 3.0 add_dynamic-update-slice_fusion.6
  132.9 2.7 select_reduce_fusion.5
  137.4 2.8 add_dynamic-update-slice_fusion.5
  140.3 2.7 select_reduce_fusion.4
  144.8 2.8 add_dynamic-update-slice_fusion.4
  147.6 2.7 select_reduce_fusion.3
  150.4 1.7 fusion.9
  152.1 3.0 add_dynamic-update-slice_fusion.3
  155.2 2.7 select_reduce_fusion.2
  159.7 2.8 add_dynamic-update-slice_fusion.2
  162.5 2.7 select_reduce_fusion.1
  167.0 3.2 add_dynamic-update-slice_fusion.1
  170.2 2.7 select_reduce_fusion
  173.0 1.7 fusion.15
  174.8 2.8 add_dynamic-update-slice_fusion
  178.8 87.1 %conditional.3 = (f32[4096,8]{0,1:T(8,128)S(1)}, f32[4096,8]{0,1:T(8,128)S(1)}, f32[4096,8,128]{2,0,1:T(8,128)}) conditional(s32[]{:T(128)} %convert_element_type.94, (f32[4096,8]{0,1:T(8,128)S(1)}, s32[4096]{0:T(1024)S(1)}, s32[]{:T(128)}, s32[]{:T(128)}, s32[32768]{0:T(1024)S(1)}, /*index=5*/s32[512]{0:T(512)S(1)}, s32[4096]{0:T(1024)S(1)}, ...), branch_computations={%region_19.36_spmd, %region_36.37_spmd} | conditional | flops 8789229568 | bytes 373268608 | solution.py:111
  178.8 5.7 copy-done.2
  184.6 2.0 compare_and_fusion.8
  186.6 11.9 %copy.60 = bf16[4096,8,128]{2,0,1:T(8,128)(2,1)} copy(bf16[4096,8,128]{0,2,1:T(8,128)(2,1)} %get-tuple-element.147) | data formatting | bytes 16777216 | tf_op jit(solution)/shard_map
  198.6 2.9 select_reduce_fusion.15
  201.5 1.7 fusion.105
  204.8 4.8 add_dynamic-update-slice_fusion.15
  212.9 5.0 add_dynamic-update-slice_fusion.14
  221.3 4.8 add_dynamic-update-slice_fusion.13
  229.4 5.2 add_dynamic-update-slice_fusion.12
  237.9 4.8 add_dynamic-update-slice_fusion.11
  246.0 5.0 add_dynamic-update-slice_fusion.10
  254.3 4.8 add_dynamic-update-slice_fusion.9
  260.9 4.8 add_dynamic-update-slice_fusion.8
  266.6 62.7 %all-gather.6.cloned.1.call-done = bf16[131072,8]{0,1:T(8,128)(2,1)} async-done(((bf16[4096,8]{0,1:T(8,128)(2,1)}), bf16[131072,8]{0,1:T(8,128)(2,1)}) %all-gather.6.cloned.1.call-update) | async-done | bytes 2097168 | tf_op jit(solution)/shard_map/all_gather | solution.py:23
  329.3 1.9 reduce_max.171
  331.3 7.6 %multiply_convert_fusion = bf16[4096,8,128]{2,0,1:T(8,128)(2,1)S(1)} fusion(f32[4096,8,128]{2,0,1:T(8,128)} %get-tuple-element.112, f32[4096,8]{0,1:T(8,128)S(1)} %get-tuple-element.184), kind=kLoop, calls=%fused_computation.305 | loop fusion | flops 8388608 | bytes 25296896 | tf_op jit(solution)/shard_map/convert_element_type | solution.py:149
  338.9 25.1 %copy.61 = bf16[4096,8,128]{2,1,0:T(8,128)(2,1)} copy(bf16[4096,8,128]{2,0,1:T(8,128)(2,1)S(1)} %multiply_convert_fusion) | data formatting | bytes 16777216 | tf_op jit(solution)/shard_map/convert_element_type | solution.py:149
  364.0 8.7 %reshape_reshape.6 = bf16[32,131072]{1,0:T(8,128)(2,1)} reshape(bf16[4096,8,128]{2,1,0:T(8,128)(2,1)} %copy.61) | data formatting | bytes 16777216 | tf_op jit(solution)/shard_map/reshape;reshape | solution.py:34
  374.7 11.2 %pad_maximum_fusion = bf16[32,132096]{1,0:T(8,128)(2,1)} fusion(bf16[32,1024]{1,0:T(8,128)(2,1)S(1)} %reshape_reshape.7, bf16[32,131072]{1,0:T(8,128)(2,1)} %reshape_reshape.6), kind=kLoop, calls=%fused_computation.306 | loop fusion | flops 16908288 | bytes 16908288 | tf_op jit(solution)/shard_map/concatenate | solution.py:34
  385.8 8.9 %reshape.816 = bf16[33024,128]{1,0:T(8,128)(2,1)} reshape(bf16[32,132096]{1,0:T(8,128)(2,1)} %pad_maximum_fusion) | data formatting | bytes 16908288 | tf_op jit(solution)/shard_map/reshape | solution.py:36
  396.6 244.6 %all-reduce.3.cloned.1.call-done = bf16[33024,128]{1,0:T(8,128)(2,1)} async-done(((bf16[33024,128]{1,0:T(8,128)(2,1)}), bf16[33024,128]{1,0:T(8,128)(2,1)}) %all-reduce.3.cloned.1.call-update) | async-done | bytes 8454160
  (86 shorter events, 41.4 us)
Async XLA Ops:
  6.5 2.7 copy-start
  6.5 97.6 %all-gather.4.cloned.1.call-start = ((), (), s32[]{:S(2)}) async-start(), calls=%async_computation | async-start | bytes 8650752 | tf_op jit(solution)/shard_map/all_gather | solution.py:121
  8.4 321.0 %all-gather.6.cloned.1.call-start = ((), (), s32[]{:S(2)}) async-start(), calls=%async_computation.1 | async-start | bytes 2162688 | tf_op jit(solution)/shard_map/all_gather | solution.py:23
  9.3 27.3 %copy-start.3 = (bf16[128,128]{1,0:T(8,128)(2,1)S(1)}, bf16[128,128]{1,0:T(8,128)(2,1)}, u32[]{:S(2)}) copy-start(bf16[128,128]{1,0:T(8,128)(2,1)} %param.10) | copy-start | bytes 98308
  9.3 27.3 %copy-start.4 = (bf16[128,128]{1,0:T(8,128)(2,1)S(1)}, bf16[128,128]{1,0:T(8,128)(2,1)}, u32[]{:S(2)}) copy-start(bf16[128,128]{1,0:T(8,128)(2,1)} %param.9) | copy-start | bytes 98308
  178.8 5.7 copy-start.2
  198.6 4.6 copy-start.1
  266.6 374.7 %all-reduce.3.cloned.1.call-start = ((), (), s32[]{:S(2)}) async-start(), calls=%async_computation.2 | async-start | bytes 16908288
  394.7 0.7 copy-start.5
Sparse Core Ops, SparseCore 0:
  9.1 94.9 all-gather.3
  266.7 62.6 all-gather.5
  394.9 246.2 all-reduce.2
where the time goes:
time: 660 us; the launch traced here: 651 us
  waiting for transfers between devices  345 us (52%)
  local copies, waits for them, and re-layouts  103 us (16%)
  matrix products  98.2 us (15%)
  other arithmetic  56.6 us (9%)
  blocking collectives  30.2 us (5%)
  between operations  16.7 us (3%)
    unnamed x4, waiting for transfers between devices  245 us
    all_gather x1, waiting for transfers between devices, over_pieces(): return lax.all_gather(array, axis).max(0)  62.7 us
    dot_general x16, matrix products, fold_block(): jnp.einsum('qhk,kd->qhd', exp_terms.astype(jnp.bfloat16), value_block, pr...  62.7 us
    all_gather x1, waiting for transfers between devices, per_device(): gathered = lax.all_gather(queries, 'row', axis=0, tiled=True)  37.2 us
    dot_general x16, matrix products, fold_block(): jnp.einsum('qhd,kd->qhk', query_mat[query_lo:query_hi], key_block, prefer...  35.5 us
    all_gather x1, blocking collectives, sent_together(): lax.all_gather(both, axis, axis=dim, tiled=True)  30.2 us
    reduce_sum x16, other arithmetic, fold_block(): jnp.sum(exp_terms, axis=2)  27.7 us
    convert_element_type x1, local copies, waits for them, and re-layouts, per_device(): (running[2] * rescale[..., None]).astype(jnp.bfloat16)  25.1 us
  transfers between devices with their start and end apart: 3, of which 3 were waited for; matrix products, arithmetic and copies ran while one was open for 4% of the time, Pallas kernels for 0%

commit v1 on v0

v1 whole, which is shorter than its diff:
```python
import functools
import math

import jax
import jax.numpy as jnp
from jax import lax
from jax.experimental import pallas as pl
from jax.experimental.pallas import tpu as pltpu
from jax.sharding import PartitionSpec as P

HQ = 8
HD = 128
ROWS = 128
TILE = 512
GROUP = 256
NEG = -1e30
SCALE = math.log2(math.e) / math.sqrt(HD)


def attend_kernel(t0_ref, seg_ref, q_ref, kv_ref, o_ref, q_scr, kv_buf, m_scr, l_scr, acc_scr, sems):
    t0 = t0_ref[0]
    seg = seg_ref[...]
    starts = [jnp.sum(jnp.where(seg < s, 1.0, 0.0)).astype(jnp.int32) for s in range(1, HQ)]
    zero = jnp.int32(0)
    lo_first, lo_last = zero, zero
    for st in starts:
        lo_first = jnp.maximum(lo_first, jnp.where(st <= t0, st, zero))
        lo_last = jnp.maximum(lo_last, jnp.where(st <= t0 + ROWS - 1, st, zero))
    high = (t0 + ROWS - 1) // TILE
    low = lo_first // TILE
    count = high - low + 1

    def fetch(i):
        at = pl.multiple_of((high - i) * TILE, TILE)
        slot = lax.rem(i, 2)
        return pltpu.make_async_copy(kv_ref.at[pl.ds(at, TILE)], kv_buf.at[slot], sems.at[slot])

    fetch(0).start()
    for h in range(HQ):
        q_scr[h * ROWS : (h + 1) * ROWS, :] = q_ref[:, h * HD : (h + 1) * HD]
    m_scr[...] = jnp.full_like(m_scr, NEG)
    l_scr[...] = jnp.zeros_like(l_scr)
    acc_scr[...] = jnp.zeros_like(acc_scr)

    def tile(i, masked):
        slot = lax.rem(i, 2)
        base = (high - i) * TILE
        k = kv_buf[slot, :, :HD]
        v = kv_buf[slot, :, HD:]
        if masked:
            t = t0 + lax.broadcasted_iota(jnp.int32, (ROWS, TILE), 0)
            u = base + lax.broadcasted_iota(jnp.int32, (ROWS, TILE), 1)
            first = jnp.zeros_like(t)
            for st in starts:
                first = jnp.maximum(first, jnp.where(st <= t, st, 0))
            seen = (u <= t) & (u >= first)
            bias = jnp.where(seen, 0.0, NEG)
            bias = jnp.concatenate([bias] * (GROUP // ROWS), axis=0)
        for g in range(HQ * ROWS // GROUP):
            rows = slice(g * GROUP, (g + 1) * GROUP)
            s = lax.dot_general(
                q_scr[rows, :], k, (((1,), (1,)), ((), ())), preferred_element_type=jnp.float32
            )
            if masked:
                s = s + bias
            parts = [s[:, c : c + 128] for c in range(0, TILE, 128)]
            top = functools.reduce(jnp.maximum, parts)
            m_old = m_scr[rows, :]
            m_new = jnp.maximum(m_old, jnp.max(top, axis=1, keepdims=True))
            alpha = jnp.exp2((m_old - m_new) * SCALE)
            m_scr[rows, :] = m_new
            shift = m_new * SCALE
            terms = [jnp.exp2(x * SCALE - shift) for x in parts]
            l_scr[rows, :] = l_scr[rows, :] * alpha + functools.reduce(jnp.add, terms)
            weights = jnp.concatenate([x.astype(jnp.bfloat16) for x in terms], axis=1)
            acc_scr[rows, :] = acc_scr[rows, :] * alpha + jnp.dot(
                weights, v, preferred_element_type=jnp.float32
            )

    def step(i, carry):
        fetch(i).wait()

        @pl.when(i + 1 < count)
        def _():
            fetch(i + 1).start()

        base = (high - i) * TILE
        partial = (base + TILE > t0) | (base < lo_last)

        @pl.when(partial)
        def _():
            tile(i, True)

        @pl.when(jnp.logical_not(partial))
        def _():
            tile(i, False)

        return carry

    lax.fori_loop(0, count, step, 0)
    for h in range(HQ):
        rows = slice(h * ROWS, (h + 1) * ROWS)
        total = jnp.sum(l_scr[rows, :], axis=1, keepdims=True)
        o_ref[:, h * HD : (h + 1) * HD] = (acc_scr[rows, :] / total).astype(jnp.bfloat16)


def attend(t0, seg, queries, kv):
    stacked = HQ * ROWS
    return pl.pallas_call(
        attend_kernel,
        out_shape=jax.ShapeDtypeStruct(queries.shape, jnp.bfloat16),
        in_specs=[
            pl.BlockSpec(memory_space=pltpu.SMEM),
            pl.BlockSpec(memory_space=pltpu.VMEM),
            pl.BlockSpec(memory_space=pltpu.VMEM),
            pl.BlockSpec(memory_space=pl.ANY),
        ],
        out_specs=pl.BlockSpec(memory_space=pltpu.VMEM),
        scratch_shapes=[
            pltpu.VMEM((stacked, HD), jnp.bfloat16),
            pltpu.VMEM((2, TILE, 2 * HD), jnp.bfloat16),
            pltpu.VMEM((stacked, 128), jnp.float32),
            pltpu.VMEM((stacked, 128), jnp.float32),
            pltpu.VMEM((stacked, HD), jnp.float32),
            pltpu.SemaphoreType.DMA((2,)),
        ],
        name="attend",
    )(t0, seg, queries, kv)


def per_device(queries, keys, values, segment_ids):
    n_row = lax.axis_size("row")
    block = lax.axis_index("col") * n_row + lax.axis_index("row")
    t0 = (block * queries.shape[0]).astype(jnp.int32).reshape(1)
    kv = lax.all_gather(jnp.concatenate([keys, values], axis=1), ("row", "col"), axis=0, tiled=True)
    return attend(t0, segment_ids.reshape(-1, 128), queries, kv)


def solution(mesh):
    in_specs = (P(("col", "row"), None), P(("row", "col"), None), P(("row", "col"), None), P())
    out_specs = P(("col", "row"), None)
    return jax.shard_map(
        per_device, mesh=mesh, in_specs=in_specs, out_specs=out_specs, check_vma=False
    )
```

time: 660 us -> 766 us (1.16)
  waiting for transfers between devices: 345 us -> 737 us
  local copies, waits for them, and re-layouts: 103 us -> 0 us
  matrix products: 98.2 us -> 0 us
  other arithmetic: 56.6 us -> 1.41 us
  blocking collectives: 30.2 us -> 0 us
    all_gather x2 -> x1, waiting for transfers between devices: 99.9 us -> 737 us  [per_device(): lax.all_gather(jnp.concatenate([keys, values], axis=1), ('row', 'col'), a...]
    unnamed x4 -> x1, waiting for transfers between devices: 245 us -> 0.02 us
    dot_general x32 -> x0, matrix products: 98.2 us -> none  [the longest x16 62.7 us: fold_block(): jnp.einsum('qhk,kd->qhd', exp_terms.astype(jnp.bfloat16), value_block, pr...]
    another operation x4 -> x0, local copies, waits for them, and re-layouts: 34 us -> none
    all_gather x1 -> x0, blocking collectives: 30.2 us -> none  [sent_together(): lax.all_gather(both, axis, axis=dim, tiled=True)]
    reduce_sum x16 -> x0, other arithmetic: 27.7 us -> none  [fold_block(): jnp.sum(exp_terms, axis=2)]
    convert_element_type x4 -> x0, local copies, waits for them, and re-layouts: 25.8 us -> none  [the longest x1 25.1 us: per_device(): (running[2] * rescale[..., None]).astype(jnp.bfloat16)]
    gather x1 -> x0, local copies, waits for them, and re-layouts: 23 us -> none  [per_device(): query_seg = jnp.take(segment_ids, query_pos)]
  transfers between devices with their start and end apart: 3 -> 1, of which waited for: 3 -> 1; matrix products, arithmetic and copies ran while one was open for 4% -> 0% of each run, Pallas kernels for 0% -> 0%
where the time goes in v1:
time: 766 us; the launch traced here: 756 us
  waiting for transfers between devices  737 us (96%)
  between operations  13.4 us (2%)
    all_gather x1, waiting for transfers between devices, per_device(): lax.all_gather(jnp.concatenate([keys, values], axis=1), ('row', 'col'), a...  737 us
  transfers between devices with their start and end apart: 1, of which 1 were waited for; matrix products, arithmetic and copies ran while one was open for 0% of the time, Pallas kernels for 0%

profile of v1, /device:TPU:1, one launch (start us, length us, event | category | flops | bytes accessed | tf_op | source)
XLA Modules:
  0.0 756.2 jit_solution(14861144486298574661)
XLA Ops:
  6.5 0.0 all-gather.2.cloned.1.call-start
  6.5 1.4 pad_maximum_fusion
  7.9 0.0 all-gather.2.cloned.1.call-update
  8.0 737.0 %all-gather.2.cloned.1.call-done.kv_ref = bf16[32768,256]{1,0:T(8,128)(2,1)} async-done(((bf16[128,256]{1,0:T(8,128)(2,1)}), bf16[32768,256]{1,0:T(8,128)(2,1)}) %all-gather.2.cloned.1.call-update) | async-done | bytes 16777232 | tf_op jit(solution)/shard_map/all_gather | solution.py:135
  744.9 4.4 attend.1
Async XLA Ops:
  6.5 738.4 %all-gather.2.cloned.1.call-start = ((), (), s32[]{:S(2)}) async-start(), calls=%async_computation | async-start | bytes 16842752 | tf_op jit(solution)/shard_map/all_gather | solution.py:135
Sparse Core Ops, SparseCore 0:
  9.2 735.6 all-gather.1

commit v2 on v1

v2 whole, which is shorter than its diff:
```python
import functools
import math

import jax
import jax.numpy as jnp
from jax import lax
from jax.experimental import pallas as pl
from jax.experimental.pallas import tpu as pltpu
from jax.sharding import PartitionSpec as P

HQ = 8
HD = 128
ROWS = 128
NZ = 8
NY = 4
GROUP = 256
NEG = -1e30
SCALE = math.log2(math.e) / math.sqrt(HD)
MESH = pl.DeviceIdType.MESH


def place():
    row, col = lax.axis_index("row"), lax.axis_index("col")
    core = lax.rem(row, 2)
    z = lax.rem(lax.div(row, 2), NZ)
    y = lax.rem(col, 2) * 2 + lax.div(row, 2 * NZ)
    x = lax.div(col, 2)
    return row, col, x, y, z, core


def exchange_kernel(
    k_ref, v_ref, win, p0_send, p0_recv, z_send, y_send, d_send, own_recv, pair_recv
):
    row, col, x, y, z, core = place()

    def device(yy, zz, cc):
        return (lax.rem(yy, 2) * NZ + zz) * 2 + cc, x * 2 + lax.div(yy, 2)

    held = row * 8 + col
    to_row = lax.rem(held, 32)
    to_z, to_core = lax.rem(lax.div(to_row, 2), NZ), lax.rem(to_row, 2)

    def first(i, target):
        zz, cc = (to_z, to_core) if target else (z, core)
        to_col = lax.rem(lax.div(held, 32) + i, 8)
        same = (to_row == row) & (to_col == col)
        out = []
        for n, ref in enumerate((k_ref, v_ref)):
            spot = win.at[2 * i, zz, cc, n]
            far = pltpu.make_async_remote_copy(
                ref, spot, p0_send.at[i, n], p0_recv.at[i, n], (to_row, to_col), MESH
            )
            near = pltpu.make_async_copy(ref, spot, p0_recv.at[i, n])
            out.append((far, near))
        return same, out

    def ring(d, zb, way, hop):
        to = lax.rem(z + (1 if way == 0 else NZ - 1), NZ)
        spot = win.at[d, zb, core]
        return pltpu.make_async_remote_copy(
            spot, spot, z_send.at[d // 2, way, hop], own_recv.at[d, zb], device(y, to, core), MESH
        )

    def across(d, zb, way):
        to = lax.rem(y + (1 if way == 0 else NY - 1), NY)
        return pltpu.make_async_remote_copy(
            win.at[d, zb, core],
            win.at[1 if way == 0 else 3, zb, core],
            y_send.at[way, zb],
            own_recv.at[1 if way == 0 else 3, zb],
            device(to, z, core),
            MESH,
        )

    def share(d, zb, mine):
        spot = win.at[d, zb, core if mine else 1 - core]
        return pltpu.make_async_remote_copy(
            spot, spot, d_send.at[d, zb], pair_recv.at[d, zb], device(y, z, 1 - core), MESH
        )

    def arrived(d, zb):
        spot = win.at[d, zb, core]
        pltpu.make_async_remote_copy(
            spot, spot, z_send.at[0, 0, 0], own_recv.at[d, zb], device(y, z, 1 - core), MESH
        ).wait_recv()

    def needed(d, zb):
        return zb <= z if d == 0 else zb >= z if d == 4 else None

    def maybe(cond, act):
        if cond is None:
            act()
        else:
            pl.when(cond)(act)

    def have(d, zb):
        if d == 0:
            pl.when(y < 3)(lambda: across(0, zb, 0).start())
            pl.when(y == 0)(lambda: across(0, zb, 1).start())
        if d == 4:
            pl.when(y == 3)(lambda: across(4, zb, 0).start())
            pl.when(y > 0)(lambda: across(4, zb, 1).start())
        maybe(needed(d, zb), lambda: share(d, zb, True).start())

    for i in (0, 2, 1):
        same, copies = first(i, True)
        for far, near in copies:
            pl.when(same)(lambda near=near: near.start())
            pl.when(jnp.logical_not(same))(lambda far=far: far.start())
    even = [lax.rem(core + e, 2) == 0 for e in range(3)]
    odd = [jnp.logical_not(e) for e in even]
    for i in (0, 2, 1):
        same, copies = first(i, False)
        for far, near in copies:
            pl.when(same)(lambda near=near: near.wait())
            pl.when(jnp.logical_not(same))(lambda far=far: far.wait_recv())
        ring(2 * i, z, 0, 0).start()
        ring(2 * i, z, 1, 0).start()
        have(2 * i, z)

    def later(zb):
        for d in (1, 3):
            arrived(d, zb)
            share(d, zb, True).start()

    for hop in range(1, 4):
        up, down = lax.rem(z + NZ - hop, NZ), lax.rem(z + hop, NZ)
        for i in (0, 2, 1):
            d = 2 * i
            arrived(d, up)
            maybe(None if hop < 3 else even[i], lambda: ring(d, up, 0, hop).start())
            have(d, up)
            arrived(d, down)
            maybe(None if hop < 3 else odd[i], lambda: ring(d, down, 1, hop).start())
            have(d, down)
        if hop == 1:
            later(z)
        else:
            later(lax.rem(z + NZ - hop + 1, NZ))
            later(lax.rem(z + hop - 1, NZ))
    last = lax.rem(z + 4, NZ)
    for i in (0, 2, 1):
        arrived(2 * i, last)
        have(2 * i, last)
    later(lax.rem(z + 5, NZ))
    later(lax.rem(z + 3, NZ))
    later(last)

    for d in range(5):
        for s in range(NZ):
            zb = lax.rem(z + s, NZ)
            maybe(needed(d, zb), lambda: share(d, zb, False).wait_recv())
            maybe(needed(d, zb), lambda: share(d, zb, True).wait_send())
    for i in range(3):
        same, copies = first(i, True)
        for far, near in copies:
            pl.when(jnp.logical_not(same))(lambda far=far: far.wait_send())
        for hop in range(4):
            up, down = lax.rem(z + NZ - hop, NZ), lax.rem(z + hop, NZ)
            maybe(None if hop < 3 else even[i], lambda: ring(2 * i, up, 0, hop).wait_send())
            maybe(None if hop < 3 else odd[i], lambda: ring(2 * i, down, 1, hop).wait_send())
    for zb in range(NZ):
        across(0, zb, 0).wait_send()
        across(0, zb, 1).wait_send()


def exchange(keys, values):
    return pl.pallas_call(
        exchange_kernel,
        out_shape=jax.ShapeDtypeStruct((5, NZ, 2, 2, ROWS, HD), jnp.bfloat16),
        in_specs=[pl.BlockSpec(memory_space=pl.ANY)] * 2,
        out_specs=pl.BlockSpec(memory_space=pltpu.VMEM),
        scratch_shapes=[
            pltpu.SemaphoreType.DMA((3, 2)),
            pltpu.SemaphoreType.DMA((3, 2)),
            pltpu.SemaphoreType.DMA((3, 2, 4)),
            pltpu.SemaphoreType.DMA((2, NZ)),
            pltpu.SemaphoreType.DMA((5, NZ)),
            pltpu.SemaphoreType.DMA((5, NZ)),
            pltpu.SemaphoreType.DMA((5, NZ)),
        ],
        compiler_params=pltpu.CompilerParams(has_side_effects=True),
        name="exchange",
    )(keys, values)


def attend_kernel(seg_ref, q_ref, win, o_ref, q_scr, m_scr, l_scr, acc_scr):
    row, col, x, y, z, core = place()
    t0 = (col * 32 + row) * ROWS
    band = (4 * x + y) * 16
    seg = seg_ref[...]
    starts = [jnp.sum(jnp.where(seg < s, 1.0, 0.0)).astype(jnp.int32) for s in range(1, HQ)]
    zero = jnp.int32(0)
    lo_first, lo_last = zero, zero
    for st in starts:
        lo_first = jnp.maximum(lo_first, jnp.where(st <= t0, st, zero))
        lo_last = jnp.maximum(lo_last, jnp.where(st <= t0 + ROWS - 1, st, zero))

    for h in range(HQ):
        q_scr[h * ROWS : (h + 1) * ROWS, :] = q_ref[:, h * HD : (h + 1) * HD]
    m_scr[...] = jnp.full_like(m_scr, NEG)
    l_scr[...] = jnp.zeros_like(l_scr)
    acc_scr[...] = jnp.zeros_like(acc_scr)

    def tile(pairs, masked):
        blocks = [(d, zb, cc) for d, zb in pairs for cc in (0, 1)]
        k = jnp.concatenate([win[d, zb, cc, 0] for d, zb, cc in blocks], axis=0)
        v = jnp.concatenate([win[d, zb, cc, 1] for d, zb, cc in blocks], axis=0)
        if masked:
            t = t0 + lax.broadcasted_iota(jnp.int32, (ROWS, 128), 0)
            lane = lax.broadcasted_iota(jnp.int32, (ROWS, 128), 1)
            start = jnp.zeros_like(t)
            for st in starts:
                start = jnp.maximum(start, jnp.where(st <= t, st, 0))
            biases = []
            for d, zb, cc in blocks:
                u = lane + (band - 16 * d + 2 * zb + cc) * ROWS
                bias = jnp.where((u <= t) & (u >= start), 0.0, NEG)
                biases.append(jnp.concatenate([bias] * (GROUP // ROWS), axis=0))
        for g in range(HQ * ROWS // GROUP):
            rows = slice(g * GROUP, (g + 1) * GROUP)
            s = lax.dot_general(
                q_scr[rows, :], k, (((1,), (1,)), ((), ())), preferred_element_type=jnp.float32
            )
            parts = [s[:, n * 128 : n * 128 + 128] for n in range(len(blocks))]
            if masked:
                parts = [p + b for p, b in zip(parts, biases)]
            top = functools.reduce(jnp.maximum, parts)
            m_old = m_scr[rows, :]
            m_new = jnp.maximum(m_old, jnp.max(top, axis=1, keepdims=True))
            alpha = jnp.exp2((m_old - m_new) * SCALE)
            m_scr[rows, :] = m_new
            shift = m_new * SCALE
            terms = [jnp.exp2(p * SCALE - shift) for p in parts]
            l_scr[rows, :] = l_scr[rows, :] * alpha + functools.reduce(jnp.add, terms)
            weights = jnp.concatenate([p.astype(jnp.bfloat16) for p in terms], axis=1)
            acc_scr[rows, :] = acc_scr[rows, :] * alpha + jnp.dot(
                weights, v, preferred_element_type=jnp.float32
            )

    tile([(0, z)], True)

    def step(i, carry):
        a = lax.rem(z + 2 * lax.rem(i, 4) + 1, NZ)
        b = lax.rem(a + 1, NZ)
        d = lax.div(i, 4)
        da = jnp.where(d > 0, d, jnp.where(a < z, 0, 4))
        db = jnp.where(d > 0, d, jnp.where(b < z, 0, 4))
        base_a = (band - 16 * da + 2 * a) * ROWS
        base_b = (band - 16 * db + 2 * b) * ROWS
        seen = (base_a + 256 > lo_first) | (base_b + 256 > lo_first)
        clear = (base_a >= lo_last) & (base_b >= lo_last)

        @pl.when(clear)
        def _():
            tile([(da, a), (db, b)], False)

        @pl.when(seen & jnp.logical_not(clear))
        def _():
            tile([(da, a), (db, b)], True)

        return carry

    lax.fori_loop(0, 16, step, 0)
    for h in range(HQ):
        rows = slice(h * ROWS, (h + 1) * ROWS)
        total = jnp.sum(l_scr[rows, :], axis=1, keepdims=True)
        o_ref[:, h * HD : (h + 1) * HD] = (acc_scr[rows, :] / total).astype(jnp.bfloat16)


def attend(seg, queries, window):
    stacked = HQ * ROWS
    return pl.pallas_call(
        attend_kernel,
        out_shape=jax.ShapeDtypeStruct(queries.shape, jnp.bfloat16),
        in_specs=[pl.BlockSpec(memory_space=pltpu.VMEM)] * 3,
        out_specs=pl.BlockSpec(memory_space=pltpu.VMEM),
        scratch_shapes=[
            pltpu.VMEM((stacked, HD), jnp.bfloat16),
            pltpu.VMEM((stacked, 128), jnp.float32),
            pltpu.VMEM((stacked, 128), jnp.float32),
            pltpu.VMEM((stacked, HD), jnp.float32),
        ],
        name="attend",
    )(seg, queries, window)


def per_device(queries, keys, values, segment_ids):
    return attend(segment_ids.reshape(-1, 128), queries, exchange(keys, values))


def solution(mesh):
    in_specs = (P(("col", "row"), None), P(("row", "col"), None), P(("row", "col"), None), P())
    out_specs = P(("col", "row"), None)
    return jax.shard_map(
        per_device, mesh=mesh, in_specs=in_specs, out_specs=out_specs, check_vma=False
    )
```

time: 766 us -> 78 us (0.10)
  the two profiles are of different devices: /device:TPU:1 before, /device:TPU:255 now
where the time goes in v2:
time: 78 us; the launch traced here: 77.3 us
  Pallas kernels  77.3 us (99%)
    pallas_call x1, Pallas kernels, exchange(): pl.pallas_call(exchange_kernel, out_shape=jax.ShapeDtypeStruct((5, NZ, 2,...  48.9 us
    pallas_call x1, Pallas kernels, attend(): pl.pallas_call(attend_kernel, out_shape=jax.ShapeDtypeStruct(queries.shap...  28.4 us

profile of v2, /device:TPU:255, one launch (start us, length us, event | category | flops | bytes accessed | tf_op | source)
XLA Modules:
  0.0 77.3 jit_solution(14301057674542411914)
XLA Ops:
  0.0 48.9 %exchange.1.win = bf16[5,8,2,2,128,128]{5,4,3,2,1,0:T(8,128)(2,1)} custom-call(bf16[128,128]{1,0:T(8,128)(2,1)} %k_ref.1, bf16[128,128]{1,0:T(8,128)(2,1)} %v_ref.1), custom_call_target="tpu_custom_call" | custom-call | tf_op jit(solution)/shard_map/exchange/pallas_call | solution.py:168
  49.0 28.4 %attend.1 = bf16[128,1024]{1,0:T(8,128)(2,1)} custom-call(s32[256,128]{1,0:T(8,128)} %bitcast.1, bf16[128,1024]{1,0:T(8,128)(2,1)} %q_ref.1, bf16[5,8,2,2,128,128]{5,4,3,2,1,0:T(8,128)(2,1)} %exchange.1.win), custom_call_target="tpu_custom_call" | custom-call | tf_op jit(solution)/shard_map/attend/pallas_call | solution.py:273
